TPU v7x, 32 devices: a whole 2x2x4 slice. The times are simulated.
32 devices in a mesh: sy: 4 (over y, x), sx: 4 (over z), wl: 2 (over core).
Axes of the slice: x: 2, y: 2, z: 4, core: 2. Of those that a mesh axis runs over, the one named last changes fastest.
Arguments:
- interface_map: bfloat16 [8, 4, 1536, 2, 1536], P(('wl', 'sy'), 'sx'), parts along dimension 0, may hold values from -0.0625 to 0.0625
- source_trace: float32 [8, 4, 2, 64, 4, 384], P(('wl', 'sy'), 'sx'), parts along dimension 0, may hold values from -6 to 6
- restriction: float32 [8, 4, 2, 32, 4, 384], P(('wl', 'sy'), 'sx'), parts along dimension 0, may hold values from -0.02734375 to 0.02734375
- prolongation: float32 [8, 4, 2, 32, 4, 384], P(('wl', 'sy'), 'sx'), parts along dimension 0, may hold values from -0.109375 to 0.109375
- coarse_inverse: float32 [4, 32, 32], P('wl'), parts along dimension 0, may hold values from -0.75 to 0.75
Outputs:
- traces: float32 [8, 4, 2, 64, 4, 384], P(('wl', 'sy'), 'sx'), parts along dimension 0
- coarse_coef: float32 [4, 64, 32], P('wl'), parts along dimension 0
There are 2 independent parts, one for each index of `wl`. A program takes and returns all parts, laid end to end along the dimension named above; each array names one. Nothing has to cross between parts.
All inputs are finite; a program needn't handle non-finite values.
Results may differ from a plain program's by a relative error of at most 0.0025.
Values sent between devices are 32-bit elements; how exact they have to be, the bound alone decides.
A program may use at most 128 MiB of HBM per device.

v0:
```python
import jax
import jax.numpy as jnp
from jax import lax
from jax.sharding import PartitionSpec as P

ITERS = 6
PRECISE = lax.Precision.HIGHEST


def shifted(value, axis, by):
    peers = lax.axis_size(axis)
    pairs = [(i, i + by) for i in range(peers) if 0 <= i + by < peers]
    return lax.ppermute(value, axis, pairs)


def with_halo(value, sides, width):
    for axis, dim in sides:
        peers, length = (lax.axis_size(axis), value.shape[dim])
        up = [(i, (i + 1) % peers) for i in range(peers - 1)]
        down = [(j, i) for i, j in up]
        last = lax.slice_in_dim(value, length - width, length, axis=dim)
        initial = lax.slice_in_dim(value, 0, width, axis=dim)
        before = lax.ppermute(last, axis, up)
        after = lax.ppermute(initial, axis, down)
        value = jnp.concatenate([before, value, after], axis=dim)
    return value


def complex_pair(left_real, left_imag, right_real, right_imag, pattern):
    real_part = jnp.einsum(pattern, left_real, right_real, precision=PRECISE) - jnp.einsum(
        pattern, left_imag, right_imag, precision=PRECISE
    )
    imag_part = jnp.einsum(pattern, left_real, right_imag, precision=PRECISE) + jnp.einsum(
        pattern, left_imag, right_real, precision=PRECISE
    )
    return jnp.stack([real_part, imag_part])


def corner_values(outgoing):
    corner_northwest = outgoing[..., 0, 0] + outgoing[..., 2, 0]
    corner_northeast = outgoing[..., 0, -1] + outgoing[..., 3, 0]
    corner_southwest = outgoing[..., 1, 0] + outgoing[..., 2, -1]
    corner_southeast = outgoing[..., 1, -1] + outgoing[..., 3, -1]
    return (corner_northwest, corner_northeast, corner_southwest, corner_southeast)


def assemble(
    from_north,
    from_south,
    from_west,
    from_east,
    into_northwest,
    into_northeast,
    into_southwest,
    into_southeast,
):
    north_side = (
        from_north.at[..., 0].add(0.5 * into_northwest).at[..., -1].add(0.5 * into_northeast)
    )
    south_side = (
        from_south.at[..., 0].add(0.5 * into_southwest).at[..., -1].add(0.5 * into_southeast)
    )
    west_side = from_west.at[..., 0].add(0.5 * into_northwest).at[..., -1].add(0.5 * into_southwest)
    east_side = from_east.at[..., 0].add(0.5 * into_northeast).at[..., -1].add(0.5 * into_southeast)
    return jnp.stack([north_side, south_side, west_side, east_side], axis=-2)


def restrict_sum(traces, weights):
    src_count, side_len = (traces.shape[1], traces.shape[3])
    coarse_width = weights.shape[1]
    flat_traces = traces.reshape(2, src_count, 4 * side_len)
    flat_weights = weights.reshape(2, coarse_width, 4 * side_len)
    return complex_pair(
        flat_traces[0], flat_traces[1], flat_weights[0], flat_weights[1], "sk,nk->sn"
    )


def outgoing_traces(traces, map_shard, source_shard):
    src_count, side_len = (traces.shape[1], traces.shape[3])
    row_block = traces.astype(jnp.bfloat16).reshape(2 * src_count, 4 * side_len)
    map_table = map_shard.reshape(4 * side_len, 8 * side_len)
    product = jnp.dot(row_block, map_table, preferred_element_type=jnp.float32).reshape(
        2, src_count, 2, 4 * side_len
    )
    real_part = product[0, :, 0] - product[1, :, 1]
    imag_part = product[0, :, 1] + product[1, :, 0]
    return jnp.stack([real_part, imag_part]).reshape(2, src_count, 4, side_len) + source_shard


def exchange_direct(outgoing):
    from_north = shifted(outgoing[:, :, 1], "sy", 1)
    from_south = shifted(outgoing[:, :, 0], "sy", -1)
    from_west = shifted(outgoing[:, :, 3], "sx", 1)
    from_east = shifted(outgoing[:, :, 2], "sx", -1)
    corner_northwest, corner_northeast, corner_southwest, corner_southeast = corner_values(outgoing)
    corner_grid = jnp.stack(
        [
            jnp.stack([corner_northwest, corner_northeast]),
            jnp.stack([corner_southwest, corner_southeast]),
        ]
    )
    padded = with_halo(corner_grid, (("sy", 0), ("sx", 1)), 1)
    return assemble(
        from_north,
        from_south,
        from_west,
        from_east,
        padded[0, 0],
        padded[0, 3],
        padded[3, 0],
        padded[3, 3],
    )


def sender_restriction(weights):
    receive_northwest = 0.5 * (weights[:, :, 0, 0] + weights[:, :, 2, 0])
    receive_northeast = 0.5 * (weights[:, :, 0, -1] + weights[:, :, 3, 0])
    receive_southwest = 0.5 * (weights[:, :, 1, 0] + weights[:, :, 2, -1])
    receive_southeast = 0.5 * (weights[:, :, 1, -1] + weights[:, :, 3, -1])
    empty_slot = jnp.zeros_like(weights[:, :, 0])

    def spread_slot(vector):
        return jnp.broadcast_to(vector[:, :, None], empty_slot.shape)

    weight_grid = jnp.stack(
        [
            jnp.stack(
                [spread_slot(receive_northwest), weights[:, :, 0], spread_slot(receive_northeast)]
            ),
            jnp.stack([weights[:, :, 2], empty_slot, weights[:, :, 3]]),
            jnp.stack(
                [spread_slot(receive_southwest), weights[:, :, 1], spread_slot(receive_southeast)]
            ),
        ]
    )
    padded = with_halo(weight_grid, (("sy", 0), ("sx", 1)), 1)
    weight_northwest = padded[0, 0][..., 0]
    weight_northeast = padded[0, 4][..., 0]
    weight_southwest = padded[4, 0][..., 0]
    weight_southeast = padded[4, 4][..., 0]
    north_weights = padded[0, 2].at[..., 0].add(weight_northwest).at[..., -1].add(weight_northeast)
    south_weights = padded[4, 2].at[..., 0].add(weight_southwest).at[..., -1].add(weight_southeast)
    west_weights = padded[2, 0].at[..., 0].add(weight_northwest).at[..., -1].add(weight_southwest)
    east_weights = padded[2, 4].at[..., 0].add(weight_northeast).at[..., -1].add(weight_southeast)
    return jnp.stack([north_weights, south_weights, west_weights, east_weights], axis=2)


def per_device(interface_map, source_trace, restriction, prolongation, coarse_inverse):
    source_shard = source_trace[0, 0]
    weights = restriction[0, 0]
    src_count, side_len = (source_shard.shape[1], source_shard.shape[3])
    coarse_width = weights.shape[1]
    lift_flat = prolongation[0, 0].reshape(2, coarse_width, 4 * side_len)
    traces = jnp.zeros(source_shard.shape, jnp.float32)
    coef_now = jnp.zeros((2, src_count, coarse_width), jnp.float32)
    coarse_total = coef_now
    sender_weights = sender_restriction(weights)
    for sweep_index in range(ITERS):
        coef_now = complex_pair(
            coarse_total[0], coarse_total[1], coarse_inverse[0], coarse_inverse[1], "sn,nq->sq"
        )
        spread = complex_pair(coef_now[0], coef_now[1], lift_flat[0], lift_flat[1], "sn,nk->sk")
        corrected = traces + spread.reshape(traces.shape)
        outgoing = outgoing_traces(corrected, interface_map, source_shard)
        if sweep_index + 1 < ITERS:
            coarse_total = lax.psum(restrict_sum(outgoing, sender_weights), ("sy", "sx"))
        traces = exchange_direct(outgoing)
    return (traces[None, None], coef_now)


def solution(mesh):
    return jax.shard_map(
        per_device,
        mesh=mesh,
        in_specs=(
            P(("wl", "sy"), "sx", None, None, None),
            P(("wl", "sy"), "sx", None, None, None, None),
            P(("wl", "sy"), "sx", None, None, None, None),
            P(("wl", "sy"), "sx", None, None, None, None),
            P("wl", None, None),
        ),
        out_specs=(P(("wl", "sy"), "sx", None, None, None, None), P("wl", None, None)),
        check_vma=False,
    )
```

profile of v0, /device:TPU:20, one launch (start us, length us, event | category | flops | bytes accessed | tf_op | source)
XLA Modules:
  0.0 721.0 jit_solution(16520153187485234129)
XLA Ops:
  2.5 9.8 %copy.272 = bf16[192,8,2,1536]{3,1,2,0:T(8,128)(2,1)} copy(bf16[192,8,2,1536]{3,2,1,0:T(2,128)(2,1)} %bitcast.751) | data formatting | bytes 18874368
  12.3 12.7 %copy.114 = bf16[3072,1536]{1,0:T(8,128)(2,1)} copy(bf16[3072,1536]{0,1:T(8,128)(2,1)} %bitcast.726) | data formatting | bytes 18874368 | tf_op jit(solution)/shard_map/dot_general | solution.py:82
  27.2 6.8 fusion.29
  51.9 4.8 collective-permute-start.5
  71.3 4.8 collective-permute-start.9
  102.5 5.2 collective-permute-done.11
  113.1 70.4 %psum.35 = f32[2,64,32]{1,2,0:T(8,128)S(1)} all-reduce(f32[2,64,32]{1,2,0:T(8,128)S(1)} %pad_maximum_fusion.1), channel_id=1, replica_groups=mesh['sy'=4,'sx'=4,'wl'=2] {'sy','sx'}, use_global_device_ids=true, to_apply=%region_0.0 | all-reduce | flops 4096 | bytes 32768 | tf_op jit(solution)/shard_map/psum | solution.py:166
  188.5 6.8 fusion.40
  198.8 72.4 %psum.36 = f32[2,64,32]{1,2,0:T(8,128)S(1)} all-reduce(f32[2,64,32]{1,2,0:T(8,128)S(1)} %pad_maximum_fusion.2), channel_id=1, replica_groups=mesh['sy'=4,'sx'=4,'wl'=2] {'sy','sx'}, use_global_device_ids=true, to_apply=%region_1.0 | all-reduce | flops 4096 | bytes 32768 | tf_op jit(solution)/shard_map/psum | solution.py:166
  273.6 3.9 collective-permute-start.13
  287.4 4.8 collective-permute-start.17
  292.2 5.5 collective-permute-start.16
  313.6 6.8 fusion.38
  323.9 70.6 %psum.37 = f32[2,64,32]{1,2,0:T(8,128)S(1)} all-reduce(f32[2,64,32]{1,2,0:T(8,128)S(1)} %pad_maximum_fusion.3), channel_id=1, replica_groups=mesh['sy'=4,'sx'=4,'wl'=2] {'sy','sx'}, use_global_device_ids=true, to_apply=%region_2.0 | all-reduce | flops 4096 | bytes 32768 | tf_op jit(solution)/shard_map/psum | solution.py:166
  406.7 3.9 collective-permute-start.26
  410.6 4.8 collective-permute-start.25
  415.5 5.6 collective-permute-start.24
  437.1 6.8 fusion.36
  447.4 70.6 %psum.38 = f32[2,64,32]{1,2,0:T(8,128)S(1)} all-reduce(f32[2,64,32]{1,2,0:T(8,128)S(1)} %pad_maximum_fusion.4), channel_id=1, replica_groups=mesh['sy'=4,'sx'=4,'wl'=2] {'sy','sx'}, use_global_device_ids=true, to_apply=%region_3.0 | all-reduce | flops 4096 | bytes 32768 | tf_op jit(solution)/shard_map/psum | solution.py:166
  520.3 3.9 collective-permute-start.29
  530.1 3.9 collective-permute-start.34
  534.1 4.8 collective-permute-start.33
  539.0 5.5 collective-permute-start.32
  560.3 6.8 fusion.34
  570.5 70.8 %psum.39 = f32[2,64,32]{1,2,0:T(8,128)S(1)} all-reduce(f32[2,64,32]{1,2,0:T(8,128)S(1)} %pad_maximum_fusion.5), channel_id=1, replica_groups=mesh['sy'=4,'sx'=4,'wl'=2] {'sy','sx'}, use_global_device_ids=true, to_apply=%region_4.0 | all-reduce | flops 4096 | bytes 32768 | tf_op jit(solution)/shard_map/psum | solution.py:166
  643.7 3.9 collective-permute-start.37
  653.5 3.9 collective-permute-start.42
  657.4 4.8 collective-permute-start.41
  662.3 5.5 collective-permute-start.40
  678.2 6.8 fusion.32
  694.2 4.2 collective-permute-start.48
  703.4 3.9 collective-permute-start.50
  (422 shorter events, 211.6 us)
Async XLA Ops:
  36.2 43.0 %collective-permute-start.7 = (f32[2,64,384]{2,1,0:T(8,128)}, f32[2,64,384]{2,1,0:T(8,128)S(1)}, u32[]{:S(2)}, u32[]{:S(2)}) collective-permute-start(f32[2,64,384]{2,1,0:T(8,128)} %get-tuple-element.741), channel_id=1, source_target_pairs={{2,0},{4,2},{6,4},{3,1},{5,3},{7,5},{10,8},{12,10},{14,12},{11,9},... | collective-permute-start | bytes 589832 | tf_op jit(solution)/shard_map/ppermute | solution.py:13
  44.7 26.6 %collective-permute-start = (f32[2,64,384]{2,1,0:T(8,128)S(1)}, f32[2,64,384]{2,1,0:T(8,128)}, u32[]{:S(2)}, u32[]{:S(2)}) collective-permute-start(f32[2,64,384]{2,1,0:T(8,128)S(1)} %get-tuple-element.740), channel_id=1, source_target_pairs={{0,8},{8,16},{16,24},{1,9},{9,17},{17,25},{2,10},{10,18},{18,26},{... | collective-permute-start | bytes 589832 | tf_op jit(solution)/shard_map/ppermute | solution.py:13
  46.6 29.5 %collective-permute-start.6 = (f32[2,64,384]{2,1,0:T(8,128)}, f32[2,64,384]{2,1,0:T(8,128)}, u32[]{:S(2)}, u32[]{:S(2)}) collective-permute-start(f32[2,64,384]{2,1,0:T(8,128)} %get-tuple-element.743), channel_id=1, source_target_pairs={{0,2},{2,4},{4,6},{1,3},{3,5},{5,7},{8,10},{10,12},{12,14},{9,11},... | collective-permute-start | bytes 589832 | tf_op jit(solution)/shard_map/ppermute | solution.py:13
  51.9 31.4 %collective-permute-start.5 = (f32[2,64,384]{2,1,0:T(8,128)}, f32[2,64,384]{2,1,0:T(8,128)}, u32[]{:S(2)}, u32[]{:S(2)}) collective-permute-start(f32[2,64,384]{2,1,0:T(8,128)} %get-tuple-element.742), channel_id=1, source_target_pairs={{8,0},{16,8},{24,16},{9,1},{17,9},{25,17},{10,2},{18,10},{26,18},{... | collective-permute-start | bytes 589832 | tf_op jit(solution)/shard_map/ppermute | solution.py:13
  67.8 18.6 %collective-permute-start.8 = (f32[1,3,2,32,384]{4,3,2,1,0:T(8,128)}, f32[1,3,2,32,384]{4,3,2,1,0:T(8,128)S(1)}, u32[]{:S(2)}, u32[]{:S(2)}) collective-permute-start(f32[1,3,2,32,384]{4,3,2,1,0:T(8,128)} %maximum_bitcast_fusion.3), channel_id=1, source_target_pairs={{0,8},{8,16},{16,24},{1,9},{9,17},{17,25},{2,10},{10,18},{18,26},{... | collective-permute-start | bytes 884744 | tf_op jit(solution)/shard_map/ppermute | solution.py:23
  71.3 16.2 %collective-permute-start.9 = (f32[1,3,2,32,384]{4,3,2,1,0:T(8,128)}, f32[1,3,2,32,384]{4,3,2,1,0:T(8,128)S(1)}, u32[]{:S(2)}, u32[]{:S(2)}) collective-permute-start(f32[1,3,2,32,384]{4,3,2,1,0:T(8,128)} %maximum_bitcast_fusion.4), channel_id=1, source_target_pairs={{8,0},{16,8},{24,16},{9,1},{17,9},{25,17},{10,2},{18,10},{26,18},{... | collective-permute-start | bytes 884744 | tf_op jit(solution)/shard_map/ppermute | solution.py:24
  271.7 15.7 %collective-permute-start.14 = (f32[1,2,2,64]{3,2,1,0:T(2,128)S(1)}, f32[1,2,2,64]{3,2,1,0:T(2,128)S(1)}, u32[]{:S(2)}, u32[]{:S(2)}) collective-permute-start(f32[1,2,2,64]{3,2,1,0:T(2,128)S(1)} %maximum_bitcast_fusion.9), channel_id=1, source_target_pairs={{8,0},{16,8},{24,16},{9,1},{17,9},{25,17},{10,2},{18,10},{26,18},{... | collective-permute-start | bytes 3080 | tf_op jit(solution)/shard_map/ppermute | solution.py:24
  273.6 18.6 %collective-permute-start.13 = (f32[1,2,2,64]{3,2,1,0:T(2,128)S(1)}, f32[1,2,2,64]{3,2,1,0:T(2,128)S(1)}, u32[]{:S(2)}, u32[]{:S(2)}) collective-permute-start(f32[1,2,2,64]{3,2,1,0:T(2,128)S(1)} %maximum_bitcast_fusion.8), channel_id=1, source_target_pairs={{0,8},{8,16},{16,24},{1,9},{9,17},{17,25},{2,10},{10,18},{18,26},{... | collective-permute-start | bytes 3080 | tf_op jit(solution)/shard_map/ppermute | solution.py:23
  279.5 28.0 %collective-permute-start.19 = (f32[2,64,384]{2,1,0:T(8,128)}, f32[2,64,384]{2,1,0:T(8,128)S(1)}, u32[]{:S(2)}, u32[]{:S(2)}) collective-permute-start(f32[2,64,384]{2,1,0:T(8,128)} %get-tuple-element.737), channel_id=1, source_target_pairs={{2,0},{4,2},{6,4},{3,1},{5,3},{7,5},{10,8},{12,10},{14,12},{11,9},... | collective-permute-start | bytes 589832 | tf_op jit(solution)/shard_map/ppermute | solution.py:13
  283.2 21.9 %collective-permute-start.12 = (f32[2,64,384]{2,1,0:T(8,128)}, f32[2,64,384]{2,1,0:T(8,128)}, u32[]{:S(2)}, u32[]{:S(2)}) collective-permute-start(f32[2,64,384]{2,1,0:T(8,128)} %get-tuple-element.736), channel_id=1, source_target_pairs={{0,8},{8,16},{16,24},{1,9},{9,17},{17,25},{2,10},{10,18},{18,26},{... | collective-permute-start | bytes 589832 | tf_op jit(solution)/shard_map/ppermute | solution.py:13
  285.2 20.0 %collective-permute-start.18 = (f32[2,64,384]{2,1,0:T(8,128)}, f32[2,64,384]{2,1,0:T(8,128)S(1)}, u32[]{:S(2)}, u32[]{:S(2)}) collective-permute-start(f32[2,64,384]{2,1,0:T(8,128)} %get-tuple-element.739), channel_id=1, source_target_pairs={{0,2},{2,4},{4,6},{1,3},{3,5},{5,7},{8,10},{10,12},{12,14},{9,11},... | collective-permute-start | bytes 589832 | tf_op jit(solution)/shard_map/ppermute | solution.py:13
  287.4 21.5 %collective-permute-start.17 = (f32[2,64,384]{2,1,0:T(8,128)}, f32[2,64,384]{2,1,0:T(8,128)S(1)}, u32[]{:S(2)}, u32[]{:S(2)}) collective-permute-start(f32[2,64,384]{2,1,0:T(8,128)} %get-tuple-element.738), channel_id=1, source_target_pairs={{8,0},{16,8},{24,16},{9,1},{17,9},{25,17},{10,2},{18,10},{26,18},{... | collective-permute-start | bytes 589832 | tf_op jit(solution)/shard_map/ppermute | solution.py:13
  396.9 18.6 %collective-permute-start.21 = (f32[1,2,2,64]{3,2,1,0:T(2,128)S(1)}, f32[1,2,2,64]{3,2,1,0:T(2,128)S(1)}, u32[]{:S(2)}, u32[]{:S(2)}) collective-permute-start(f32[1,2,2,64]{3,2,1,0:T(2,128)S(1)} %maximum_bitcast_fusion.10), channel_id=1, source_target_pairs={{0,8},{8,16},{16,24},{1,9},{9,17},{17,25},{2,10},{10,18},{18,26},{... | collective-permute-start | bytes 3080 | tf_op jit(solution)/shard_map/ppermute | solution.py:23
  402.8 28.0 %collective-permute-start.27 = (f32[2,64,384]{2,1,0:T(8,128)}, f32[2,64,384]{2,1,0:T(8,128)S(1)}, u32[]{:S(2)}, u32[]{:S(2)}) collective-permute-start(f32[2,64,384]{2,1,0:T(8,128)} %get-tuple-element.733), channel_id=1, source_target_pairs={{2,0},{4,2},{6,4},{3,1},{5,3},{7,5},{10,8},{12,10},{14,12},{11,9},... | collective-permute-start | bytes 589832 | tf_op jit(solution)/shard_map/ppermute | solution.py:13
  404.8 23.7 %collective-permute-start.20 = (f32[2,64,384]{2,1,0:T(8,128)}, f32[2,64,384]{2,1,0:T(8,128)}, u32[]{:S(2)}, u32[]{:S(2)}) collective-permute-start(f32[2,64,384]{2,1,0:T(8,128)} %get-tuple-element.732), channel_id=1, source_target_pairs={{0,8},{8,16},{16,24},{1,9},{9,17},{17,25},{2,10},{10,18},{18,26},{... | collective-permute-start | bytes 589832 | tf_op jit(solution)/shard_map/ppermute | solution.py:13
  406.7 21.8 %collective-permute-start.26 = (f32[2,64,384]{2,1,0:T(8,128)}, f32[2,64,384]{2,1,0:T(8,128)S(1)}, u32[]{:S(2)}, u32[]{:S(2)}) collective-permute-start(f32[2,64,384]{2,1,0:T(8,128)} %get-tuple-element.735), channel_id=1, source_target_pairs={{0,2},{2,4},{4,6},{1,3},{3,5},{5,7},{8,10},{10,12},{12,14},{9,11},... | collective-permute-start | bytes 589832 | tf_op jit(solution)/shard_map/ppermute | solution.py:13
  410.6 21.5 %collective-permute-start.25 = (f32[2,64,384]{2,1,0:T(8,128)}, f32[2,64,384]{2,1,0:T(8,128)S(1)}, u32[]{:S(2)}, u32[]{:S(2)}) collective-permute-start(f32[2,64,384]{2,1,0:T(8,128)} %get-tuple-element.734), channel_id=1, source_target_pairs={{8,0},{16,8},{24,16},{9,1},{17,9},{25,17},{10,2},{18,10},{26,18},{... | collective-permute-start | bytes 589832 | tf_op jit(solution)/shard_map/ppermute | solution.py:13
  518.4 15.7 %collective-permute-start.30 = (f32[1,2,2,64]{3,2,1,0:T(2,128)S(1)}, f32[1,2,2,64]{3,2,1,0:T(2,128)S(1)}, u32[]{:S(2)}, u32[]{:S(2)}) collective-permute-start(f32[1,2,2,64]{3,2,1,0:T(2,128)S(1)} %maximum_bitcast_fusion.13), channel_id=1, source_target_pairs={{8,0},{16,8},{24,16},{9,1},{17,9},{25,17},{10,2},{18,10},{26,18},{... | collective-permute-start | bytes 3080 | tf_op jit(solution)/shard_map/ppermute | solution.py:24
  520.3 18.6 %collective-permute-start.29 = (f32[1,2,2,64]{3,2,1,0:T(2,128)S(1)}, f32[1,2,2,64]{3,2,1,0:T(2,128)S(1)}, u32[]{:S(2)}, u32[]{:S(2)}) collective-permute-start(f32[1,2,2,64]{3,2,1,0:T(2,128)S(1)} %maximum_bitcast_fusion.12), channel_id=1, source_target_pairs={{0,8},{8,16},{16,24},{1,9},{9,17},{17,25},{2,10},{10,18},{18,26},{... | collective-permute-start | bytes 3080 | tf_op jit(solution)/shard_map/ppermute | solution.py:23
  526.3 28.0 %collective-permute-start.35 = (f32[2,64,384]{2,1,0:T(8,128)}, f32[2,64,384]{2,1,0:T(8,128)S(1)}, u32[]{:S(2)}, u32[]{:S(2)}) collective-permute-start(f32[2,64,384]{2,1,0:T(8,128)} %get-tuple-element.729), channel_id=1, source_target_pairs={{2,0},{4,2},{6,4},{3,1},{5,3},{7,5},{10,8},{12,10},{14,12},{11,9},... | collective-permute-start | bytes 589832 | tf_op jit(solution)/shard_map/ppermute | solution.py:13
  528.2 23.7 %collective-permute-start.28 = (f32[2,64,384]{2,1,0:T(8,128)}, f32[2,64,384]{2,1,0:T(8,128)}, u32[]{:S(2)}, u32[]{:S(2)}) collective-permute-start(f32[2,64,384]{2,1,0:T(8,128)} %get-tuple-element.728), channel_id=1, source_target_pairs={{0,8},{8,16},{16,24},{1,9},{9,17},{17,25},{2,10},{10,18},{18,26},{... | collective-permute-start | bytes 589832 | tf_op jit(solution)/shard_map/ppermute | solution.py:13
  530.1 21.8 %collective-permute-start.34 = (f32[2,64,384]{2,1,0:T(8,128)}, f32[2,64,384]{2,1,0:T(8,128)S(1)}, u32[]{:S(2)}, u32[]{:S(2)}) collective-permute-start(f32[2,64,384]{2,1,0:T(8,128)} %get-tuple-element.731), channel_id=1, source_target_pairs={{0,2},{2,4},{4,6},{1,3},{3,5},{5,7},{8,10},{10,12},{12,14},{9,11},... | collective-permute-start | bytes 589832 | tf_op jit(solution)/shard_map/ppermute | solution.py:13
  534.1 21.5 %collective-permute-start.33 = (f32[2,64,384]{2,1,0:T(8,128)}, f32[2,64,384]{2,1,0:T(8,128)S(1)}, u32[]{:S(2)}, u32[]{:S(2)}) collective-permute-start(f32[2,64,384]{2,1,0:T(8,128)} %get-tuple-element.730), channel_id=1, source_target_pairs={{8,0},{16,8},{24,16},{9,1},{17,9},{25,17},{10,2},{18,10},{26,18},{... | collective-permute-start | bytes 589832 | tf_op jit(solution)/shard_map/ppermute | solution.py:13
  641.7 15.7 %collective-permute-start.38 = (f32[1,2,2,64]{3,2,1,0:T(2,128)S(1)}, f32[1,2,2,64]{3,2,1,0:T(2,128)S(1)}, u32[]{:S(2)}, u32[]{:S(2)}) collective-permute-start(f32[1,2,2,64]{3,2,1,0:T(2,128)S(1)} %maximum_bitcast_fusion.15), channel_id=1, source_target_pairs={{8,0},{16,8},{24,16},{9,1},{17,9},{25,17},{10,2},{18,10},{26,18},{... | collective-permute-start | bytes 3080 | tf_op jit(solution)/shard_map/ppermute | solution.py:24
  643.7 18.6 %collective-permute-start.37 = (f32[1,2,2,64]{3,2,1,0:T(2,128)S(1)}, f32[1,2,2,64]{3,2,1,0:T(2,128)S(1)}, u32[]{:S(2)}, u32[]{:S(2)}) collective-permute-start(f32[1,2,2,64]{3,2,1,0:T(2,128)S(1)} %maximum_bitcast_fusion.14), channel_id=1, source_target_pairs={{0,8},{8,16},{16,24},{1,9},{9,17},{17,25},{2,10},{10,18},{18,26},{... | collective-permute-start | bytes 3080 | tf_op jit(solution)/shard_map/ppermute | solution.py:23
  649.6 25.8 %collective-permute-start.43 = (f32[2,64,384]{2,1,0:T(8,128)S(1)}, f32[2,64,384]{2,1,0:T(8,128)S(1)}, u32[]{:S(2)}, u32[]{:S(2)}) collective-permute-start(f32[2,64,384]{2,1,0:T(8,128)S(1)} %get-tuple-element.725), channel_id=1, source_target_pairs={{2,0},{4,2},{6,4},{3,1},{5,3},{7,5},{10,8},{12,10},{14,12},{11,9},... | collective-permute-start | bytes 589832 | tf_op jit(solution)/shard_map/ppermute | solution.py:13
  651.5 23.7 %collective-permute-start.36 = (f32[2,64,384]{2,1,0:T(8,128)}, f32[2,64,384]{2,1,0:T(8,128)S(1)}, u32[]{:S(2)}, u32[]{:S(2)}) collective-permute-start(f32[2,64,384]{2,1,0:T(8,128)} %get-tuple-element.724), channel_id=1, source_target_pairs={{0,8},{8,16},{16,24},{1,9},{9,17},{17,25},{2,10},{10,18},{18,26},{... | collective-permute-start | bytes 589832 | tf_op jit(solution)/shard_map/ppermute | solution.py:13
  653.5 21.8 %collective-permute-start.42 = (f32[2,64,384]{2,1,0:T(8,128)}, f32[2,64,384]{2,1,0:T(8,128)S(1)}, u32[]{:S(2)}, u32[]{:S(2)}) collective-permute-start(f32[2,64,384]{2,1,0:T(8,128)} %get-tuple-element.727), channel_id=1, source_target_pairs={{0,2},{2,4},{4,6},{1,3},{3,5},{5,7},{8,10},{10,12},{12,14},{9,11},... | collective-permute-start | bytes 589832 | tf_op jit(solution)/shard_map/ppermute | solution.py:13
  657.4 18.5 %collective-permute-start.41 = (f32[2,64,384]{2,1,0:T(8,128)S(1)}, f32[2,64,384]{2,1,0:T(8,128)S(1)}, u32[]{:S(2)}, u32[]{:S(2)}) collective-permute-start(f32[2,64,384]{2,1,0:T(8,128)S(1)} %get-tuple-element.726), channel_id=1, source_target_pairs={{8,0},{16,8},{24,16},{9,1},{17,9},{25,17},{10,2},{18,10},{26,18},{... | collective-permute-start | bytes 589832 | tf_op jit(solution)/shard_map/ppermute | solution.py:13
  694.2 16.9 %collective-permute-start.48 = (f32[4,1,2,64]{3,2,1,0:T(2,128)S(1)}, f32[4,1,2,64]{3,2,1,0:T(2,128)S(1)}, u32[]{:S(2)}, u32[]{:S(2)}) collective-permute-start(f32[4,1,2,64]{3,2,1,0:T(2,128)S(1)} %get-tuple-element.813), channel_id=1, source_target_pairs={{2,0},{4,2},{6,4},{3,1},{5,3},{7,5},{10,8},{12,10},{14,12},{11,9},... | collective-permute-start | bytes 6152 | tf_op jit(solution)/shard_map/ppermute | solution.py:24
  698.4 18.7 %collective-permute-start.51 = (f32[2,64,384]{2,1,0:T(8,128)S(1)}, f32[2,64,384]{2,1,0:T(8,128)S(1)}, u32[]{:S(2)}, u32[]{:S(2)}) collective-permute-start(f32[2,64,384]{2,1,0:T(8,128)S(1)} %get-tuple-element.722), channel_id=1, source_target_pairs={{2,0},{4,2},{6,4},{3,1},{5,3},{7,5},{10,8},{12,10},{14,12},{11,9},... | collective-permute-start | bytes 589832 | tf_op jit(solution)/shard_map/ppermute | solution.py:13
  700.4 16.5 %collective-permute-start.44 = (f32[2,64,384]{2,1,0:T(8,128)S(1)}, f32[2,64,384]{2,1,0:T(8,128)S(1)}, u32[]{:S(2)}, u32[]{:S(2)}) collective-permute-start(f32[2,64,384]{2,1,0:T(8,128)S(1)} %get-tuple-element.720), channel_id=1, source_target_pairs={{0,8},{8,16},{16,24},{1,9},{9,17},{17,25},{2,10},{10,18},{18,26},{... | collective-permute-start | bytes 589832 | tf_op jit(solution)/shard_map/ppermute | solution.py:13
  (26 other events, 282.9 us)
where the time goes:
time: 732 us; the launch traced here: 721 us
  blocking collectives  355 us (48%)
  starting transfers between devices  163 us (22%)
  local copies, waits for them, and re-layouts  74.8 us (10%)
  matrix products  67.9 us (9%)
  waiting for transfers between devices  32.1 us (4%)
  other arithmetic  24.6 us (3%)
    psum x5, blocking collectives, per_device(): lax.psum(restrict_sum(outgoing, sender_weights), ('sy', 'sx'))  355 us
    ppermute x24, starting transfers between devices, shifted(): return lax.ppermute(value, axis, pairs)  75.5 us
    ppermute x14, starting transfers between devices, with_halo(): after = lax.ppermute(initial, axis, down)  50.4 us
    dot_general x6, matrix products, outgoing_traces(): jnp.dot(row_block, map_table, preferred_element_type=jnp.float32)  40.6 us
    ppermute x14, starting transfers between devices, with_halo(): before = lax.ppermute(last, axis, up)  37.3 us
    ppermute x14, waiting for transfers between devices, with_halo(): before = lax.ppermute(last, axis, up)  23 us
  transfers between devices with their start and end apart: 52, of which 13 were waited for; matrix products, arithmetic and copies ran while one was open for 7% of the time, Pallas kernels for 0%

commit v1 on v0

--- a/solution.py
+++ b/solution.py
@@ -163,7 +163,8 @@
         corrected = traces + spread.reshape(traces.shape)
         outgoing = outgoing_traces(corrected, interface_map, source_shard)
         if sweep_index + 1 < ITERS:
-            coarse_total = lax.psum(restrict_sum(outgoing, sender_weights), ("sy", "sx"))
+            x_part = restrict_sum(outgoing, sender_weights)
+            coarse_total = lax.all_gather(x_part, ("sy", "sx")).sum(axis=0)
         traces = exchange_direct(outgoing)
     return (traces[None, None], coef_now)
 

time: 732 us -> 574 us (0.78)
  blocking collectives: 355 us -> 195 us
    psum x5 -> x0, blocking collectives: 355 us -> none  [per_device(): lax.psum(restrict_sum(outgoing, sender_weights), ('sy', 'sx'))]
    all_gather x0 -> x5, blocking collectives: none -> 195 us  [per_device(): coarse_total = lax.all_gather(x_part, ('sy', 'sx')).sum(axis=0)]
  transfers between devices with their start and end apart: 52 -> 52, of which waited for: 13 -> 13; matrix products, arithmetic and copies ran while one was open for 7% -> 9% of each run, Pallas kernels for 0% -> 0%
where the time goes in v1:
time: 574 us; the launch traced here: 563 us
  blocking collectives  195 us (34%)
  starting transfers between devices  165 us (29%)
  local copies, waits for them, and re-layouts  74.8 us (13%)
  matrix products  67.9 us (12%)
  waiting for transfers between devices  32.2 us (6%)
  other arithmetic  24.8 us (4%)
    all_gather x5, blocking collectives, per_device(): coarse_total = lax.all_gather(x_part, ('sy', 'sx')).sum(axis=0)  195 us
    ppermute x24, starting transfers between devices, shifted(): return lax.ppermute(value, axis, pairs)  82.2 us
    ppermute x14, starting transfers between devices, with_halo(): after = lax.ppermute(initial, axis, down)  50 us
    dot_general x6, matrix products, outgoing_traces(): jnp.dot(row_block, map_table, preferred_element_type=jnp.float32)  40.6 us
    ppermute x14, starting transfers between devices, with_halo(): before = lax.ppermute(last, axis, up)  32.5 us
    ppermute x14, waiting for transfers between devices, with_halo(): before = lax.ppermute(last, axis, up)  22.7 us
    scatter-add x12, local copies, waits for them, and re-layouts, assemble(): from_north.at[..., 0].add(0.5 * into_northwest).at[..., -1]  14.5 us
    dot_general x1, local copies, waits for them, and re-layouts, outgoing_traces(): jnp.dot(row_block, map_table, preferred_element_type=jnp.float32)  12.7 us
  transfers between devices with their start and end apart: 52, of which 13 were waited for; matrix products, arithmetic and copies ran while one was open for 9% of the time, Pallas kernels for 0%

profile of v1, /device:TPU:20, one launch (start us, length us, event | category | flops | bytes accessed | tf_op | source)
XLA Modules:
  0.0 563.0 jit_solution(6117901751935026167)
XLA Ops:
  2.5 9.8 %copy.404 = bf16[192,8,2,1536]{3,1,2,0:T(8,128)(2,1)} copy(bf16[192,8,2,1536]{3,2,1,0:T(2,128)(2,1)} %bitcast.756) | data formatting | bytes 18874368
  12.3 12.7 %copy.246 = bf16[3072,1536]{1,0:T(8,128)(2,1)} copy(bf16[3072,1536]{0,1:T(8,128)(2,1)} %bitcast.731) | data formatting | bytes 18874368 | tf_op jit(solution)/shard_map/dot_general | solution.py:82
  27.2 6.8 %fusion.29 = f32[2,64,2,1536]{3,1,2,0:T(8,128)S(1)} fusion(bf16[2,1536,1536,1]{2,1,0,3:T(8,128)(2,1)} %bitcast.725, bf16[1,64,1536]{2,1,0:T(8,128)(2,1)S(1)} %fusion.2, bf16[1,64,1536]{2,1,0:T(8,128)(2,1)S(1)} %fusion.3), kind=kOutput, calls=%fused_computation.106 | convolution fusion | flops 1208745984 | bytes 11403264 | tf_op jit(solution)/shard_map/dot_general | solution.py:82
  51.9 4.8 collective-permute-start.5
  71.3 4.8 collective-permute-start.9
  96.7 3.9 collective-permute-start.11
  102.5 5.2 collective-permute-done.11
  113.1 38.4 %all-gather = f32[32,64,32]{1,2,0:T(8,128)S(1)} all-gather(f32[2,64,32]{1,2,0:T(8,128)S(1)} %pad_maximum_fusion.1), channel_id=2, replica_groups=mesh['sy'=4,'sx'=4,'wl'=2] {'sy','sx'}, dimensions={0}, use_global_device_ids=true | all-gather | bytes 278528 | tf_op jit(solution)/shard_map/all_gather | solution.py:167
  156.6 6.8 %fusion.40 = f32[2,64,2,1536]{3,1,2,0:T(8,128)S(1)} fusion(bf16[2,1536,1536,1]{2,1,0,3:T(8,128)(2,1)} %bitcast.726, bf16[2,64,1536,1]{2,1,0,3:T(8,128)(2,1)S(1)} %reshape.2909), kind=kOutput, calls=%fused_computation.118 | convolution fusion | flops 1207959552 | bytes 11403264 | tf_op jit(solution)/shard_map/dot_general | solution.py:82
  166.9 42.0 %all-gather.1 = f32[32,64,32]{1,2,0:T(8,128)S(1)} all-gather(f32[2,64,32]{1,2,0:T(8,128)S(1)} %pad_maximum_fusion.2), channel_id=3, replica_groups=mesh['sy'=4,'sx'=4,'wl'=2] {'sy','sx'}, dimensions={0}, use_global_device_ids=true | all-gather | bytes 278528 | tf_op jit(solution)/shard_map/all_gather | solution.py:167
  217.3 5.8 %collective-permute-start.19 = (f32[2,64,384]{2,1,0:T(8,128)}, f32[2,64,384]{2,1,0:T(8,128)S(1)}, u32[]{:S(2)}, u32[]{:S(2)}) collective-permute-start(f32[2,64,384]{2,1,0:T(8,128)} %get-tuple-element.739), channel_id=1, source_target_pairs={{2,0},{4,2},{6,4},{3,1},{5,3},{7,5},{10,8},{12,10},{14,12},{11,9},... | collective-permute-start | bytes 589832 | tf_op jit(solution)/shard_map/ppermute | solution.py:13
  227.0 4.8 collective-permute-start.17
  231.9 4.0 collective-permute-start.16
  251.8 6.8 %fusion.38 = f32[2,64,2,1536]{3,1,2,0:T(8,128)S(1)} fusion(bf16[2,1536,1536,1]{2,1,0,3:T(8,128)(2,1)} %bitcast.727, bf16[2,64,1536,1]{2,1,0,3:T(8,128)(2,1)S(1)} %reshape.2914), kind=kOutput, calls=%fused_computation.116 | convolution fusion | flops 1207959552 | bytes 11403264 | tf_op jit(solution)/shard_map/dot_general | solution.py:82
  262.0 38.5 %all-gather.2 = f32[32,64,32]{1,2,0:T(8,128)S(1)} all-gather(f32[2,64,32]{1,2,0:T(8,128)S(1)} %pad_maximum_fusion.3), channel_id=4, replica_groups=mesh['sy'=4,'sx'=4,'wl'=2] {'sy','sx'}, dimensions={0}, use_global_device_ids=true | all-gather | bytes 278528 | tf_op jit(solution)/shard_map/all_gather | solution.py:167
  308.9 5.7 %collective-permute-start.27 = (f32[2,64,384]{2,1,0:T(8,128)}, f32[2,64,384]{2,1,0:T(8,128)S(1)}, u32[]{:S(2)}, u32[]{:S(2)}) collective-permute-start(f32[2,64,384]{2,1,0:T(8,128)} %get-tuple-element.735), channel_id=1, source_target_pairs={{2,0},{4,2},{6,4},{3,1},{5,3},{7,5},{10,8},{12,10},{14,12},{11,9},... | collective-permute-start | bytes 589832 | tf_op jit(solution)/shard_map/ppermute | solution.py:13
  318.5 4.8 collective-permute-start.25
  323.4 4.1 collective-permute-start.24
  343.5 6.8 %fusion.36 = f32[2,64,2,1536]{3,1,2,0:T(8,128)S(1)} fusion(bf16[2,1536,1536,1]{2,1,0,3:T(8,128)(2,1)} %bitcast.728, bf16[2,64,1536,1]{2,1,0,3:T(8,128)(2,1)S(1)} %reshape.2919), kind=kOutput, calls=%fused_computation.114 | convolution fusion | flops 1207959552 | bytes 11403264 | tf_op jit(solution)/shard_map/dot_general | solution.py:82
  353.8 37.8 %all-gather.3 = f32[32,64,32]{1,2,0:T(8,128)S(1)} all-gather(f32[2,64,32]{1,2,0:T(8,128)S(1)} %pad_maximum_fusion.4), channel_id=5, replica_groups=mesh['sy'=4,'sx'=4,'wl'=2] {'sy','sx'}, dimensions={0}, use_global_device_ids=true | all-gather | bytes 278528 | tf_op jit(solution)/shard_map/all_gather | solution.py:167
  400.0 5.7 %collective-permute-start.35 = (f32[2,64,384]{2,1,0:T(8,128)}, f32[2,64,384]{2,1,0:T(8,128)S(1)}, u32[]{:S(2)}, u32[]{:S(2)}) collective-permute-start(f32[2,64,384]{2,1,0:T(8,128)} %get-tuple-element.731), channel_id=1, source_target_pairs={{2,0},{4,2},{6,4},{3,1},{5,3},{7,5},{10,8},{12,10},{14,12},{11,9},... | collective-permute-start | bytes 589832 | tf_op jit(solution)/shard_map/ppermute | solution.py:13
  409.6 4.8 collective-permute-start.33
  414.4 4.1 collective-permute-start.32
  434.4 6.8 %fusion.34 = f32[2,64,2,1536]{3,1,2,0:T(8,128)S(1)} fusion(bf16[2,1536,1536,1]{2,1,0,3:T(8,128)(2,1)} %bitcast.729, bf16[2,64,1536,1]{2,1,0,3:T(8,128)(2,1)S(1)} %reshape.2924), kind=kOutput, calls=%fused_computation.112 | convolution fusion | flops 1207959552 | bytes 11403264 | tf_op jit(solution)/shard_map/dot_general | solution.py:82
  444.5 38.2 %all-gather.4 = f32[32,64,32]{1,2,0:T(8,128)S(1)} all-gather(f32[2,64,32]{1,2,0:T(8,128)S(1)} %pad_maximum_fusion.5), channel_id=6, replica_groups=mesh['sy'=4,'sx'=4,'wl'=2] {'sy','sx'}, dimensions={0}, use_global_device_ids=true | all-gather | bytes 278528 | tf_op jit(solution)/shard_map/all_gather | solution.py:167
  491.1 4.9 collective-permute-start.43
  499.9 4.8 collective-permute-start.41
  504.8 5.0 collective-permute-start.40
  520.2 6.8 %fusion.32 = f32[2,64,2,1536]{3,1,2,0:T(8,128)S(1)} fusion(bf16[2,1536,1536,1]{2,1,0,3:T(8,128)(2,1)} %bitcast.730, bf16[2,64,1536,1]{2,1,0,3:T(8,128)(2,1)S(1)} %reshape.2929), kind=kOutput, calls=%fused_computation.110 | convolution fusion | flops 1207959552 | bytes 11403264 | tf_op jit(solution)/shard_map/dot_general | solution.py:82
  529.8 3.9 collective-permute-start.45
  536.2 3.9 collective-permute-start.48
  545.3 3.9 collective-permute-start.50
  (427 shorter events, 212.1 us)
Async XLA Ops:
  36.2 43.0 %collective-permute-start.7 = (f32[2,64,384]{2,1,0:T(8,128)}, f32[2,64,384]{2,1,0:T(8,128)S(1)}, u32[]{:S(2)}, u32[]{:S(2)}) collective-permute-start(f32[2,64,384]{2,1,0:T(8,128)} %get-tuple-element.743), channel_id=1, source_target_pairs={{2,0},{4,2},{6,4},{3,1},{5,3},{7,5},{10,8},{12,10},{14,12},{11,9},... | collective-permute-start | bytes 589832 | tf_op jit(solution)/shard_map/ppermute | solution.py:13
  44.7 26.6 %collective-permute-start = (f32[2,64,384]{2,1,0:T(8,128)S(1)}, f32[2,64,384]{2,1,0:T(8,128)}, u32[]{:S(2)}, u32[]{:S(2)}) collective-permute-start(f32[2,64,384]{2,1,0:T(8,128)S(1)} %get-tuple-element.742), channel_id=1, source_target_pairs={{0,8},{8,16},{16,24},{1,9},{9,17},{17,25},{2,10},{10,18},{18,26},{... | collective-permute-start | bytes 589832 | tf_op jit(solution)/shard_map/ppermute | solution.py:13
  46.6 29.5 %collective-permute-start.6 = (f32[2,64,384]{2,1,0:T(8,128)}, f32[2,64,384]{2,1,0:T(8,128)}, u32[]{:S(2)}, u32[]{:S(2)}) collective-permute-start(f32[2,64,384]{2,1,0:T(8,128)} %get-tuple-element.745), channel_id=1, source_target_pairs={{0,2},{2,4},{4,6},{1,3},{3,5},{5,7},{8,10},{10,12},{12,14},{9,11},... | collective-permute-start | bytes 589832 | tf_op jit(solution)/shard_map/ppermute | solution.py:13
  51.9 31.4 %collective-permute-start.5 = (f32[2,64,384]{2,1,0:T(8,128)}, f32[2,64,384]{2,1,0:T(8,128)}, u32[]{:S(2)}, u32[]{:S(2)}) collective-permute-start(f32[2,64,384]{2,1,0:T(8,128)} %get-tuple-element.744), channel_id=1, source_target_pairs={{8,0},{16,8},{24,16},{9,1},{17,9},{25,17},{10,2},{18,10},{26,18},{... | collective-permute-start | bytes 589832 | tf_op jit(solution)/shard_map/ppermute | solution.py:13
  67.8 18.6 %collective-permute-start.8 = (f32[1,3,2,32,384]{4,3,2,1,0:T(8,128)}, f32[1,3,2,32,384]{4,3,2,1,0:T(8,128)S(1)}, u32[]{:S(2)}, u32[]{:S(2)}) collective-permute-start(f32[1,3,2,32,384]{4,3,2,1,0:T(8,128)} %maximum_bitcast_fusion.3), channel_id=1, source_target_pairs={{0,8},{8,16},{16,24},{1,9},{9,17},{17,25},{2,10},{10,18},{18,26},{... | collective-permute-start | bytes 884744 | tf_op jit(solution)/shard_map/ppermute | solution.py:23
  209.4 17.6 %collective-permute-start.14 = (f32[1,2,2,64]{3,2,1,0:T(2,128)S(1)}, f32[1,2,2,64]{3,2,1,0:T(2,128)S(1)}, u32[]{:S(2)}, u32[]{:S(2)}) collective-permute-start(f32[1,2,2,64]{3,2,1,0:T(2,128)S(1)} %maximum_bitcast_fusion.9), channel_id=1, source_target_pairs={{8,0},{16,8},{24,16},{9,1},{17,9},{25,17},{10,2},{18,10},{26,18},{... | collective-permute-start | bytes 3080 | tf_op jit(solution)/shard_map/ppermute | solution.py:24
  212.5 19.3 %collective-permute-start.13 = (f32[1,2,2,64]{3,2,1,0:T(2,128)S(1)}, f32[1,2,2,64]{3,2,1,0:T(2,128)S(1)}, u32[]{:S(2)}, u32[]{:S(2)}) collective-permute-start(f32[1,2,2,64]{3,2,1,0:T(2,128)S(1)} %maximum_bitcast_fusion.8), channel_id=1, source_target_pairs={{0,8},{8,16},{16,24},{1,9},{9,17},{17,25},{2,10},{10,18},{18,26},{... | collective-permute-start | bytes 3080 | tf_op jit(solution)/shard_map/ppermute | solution.py:23
  217.3 28.4 %collective-permute-start.19 = (f32[2,64,384]{2,1,0:T(8,128)}, f32[2,64,384]{2,1,0:T(8,128)S(1)}, u32[]{:S(2)}, u32[]{:S(2)}) collective-permute-start(f32[2,64,384]{2,1,0:T(8,128)} %get-tuple-element.739), channel_id=1, source_target_pairs={{2,0},{4,2},{6,4},{3,1},{5,3},{7,5},{10,8},{12,10},{14,12},{11,9},... | collective-permute-start | bytes 589832 | tf_op jit(solution)/shard_map/ppermute | solution.py:13
  223.1 20.2 %collective-permute-start.12 = (f32[2,64,384]{2,1,0:T(8,128)}, f32[2,64,384]{2,1,0:T(8,128)}, u32[]{:S(2)}, u32[]{:S(2)}) collective-permute-start(f32[2,64,384]{2,1,0:T(8,128)} %get-tuple-element.738), channel_id=1, source_target_pairs={{0,8},{8,16},{16,24},{1,9},{9,17},{17,25},{2,10},{10,18},{18,26},{... | collective-permute-start | bytes 589832 | tf_op jit(solution)/shard_map/ppermute | solution.py:13
  225.1 18.2 %collective-permute-start.18 = (f32[2,64,384]{2,1,0:T(8,128)}, f32[2,64,384]{2,1,0:T(8,128)S(1)}, u32[]{:S(2)}, u32[]{:S(2)}) collective-permute-start(f32[2,64,384]{2,1,0:T(8,128)} %get-tuple-element.741), channel_id=1, source_target_pairs={{0,2},{2,4},{4,6},{1,3},{3,5},{5,7},{8,10},{10,12},{12,14},{9,11},... | collective-permute-start | bytes 589832 | tf_op jit(solution)/shard_map/ppermute | solution.py:13
  227.0 20.0 %collective-permute-start.17 = (f32[2,64,384]{2,1,0:T(8,128)}, f32[2,64,384]{2,1,0:T(8,128)S(1)}, u32[]{:S(2)}, u32[]{:S(2)}) collective-permute-start(f32[2,64,384]{2,1,0:T(8,128)} %get-tuple-element.740), channel_id=1, source_target_pairs={{8,0},{16,8},{24,16},{9,1},{17,9},{25,17},{10,2},{18,10},{26,18},{... | collective-permute-start | bytes 589832 | tf_op jit(solution)/shard_map/ppermute | solution.py:13
  301.0 17.5 %collective-permute-start.22 = (f32[1,2,2,64]{3,2,1,0:T(2,128)S(1)}, f32[1,2,2,64]{3,2,1,0:T(2,128)S(1)}, u32[]{:S(2)}, u32[]{:S(2)}) collective-permute-start(f32[1,2,2,64]{3,2,1,0:T(2,128)S(1)} %maximum_bitcast_fusion.11), channel_id=1, source_target_pairs={{8,0},{16,8},{24,16},{9,1},{17,9},{25,17},{10,2},{18,10},{26,18},{... | collective-permute-start | bytes 3080 | tf_op jit(solution)/shard_map/ppermute | solution.py:24
  304.4 18.9 %collective-permute-start.21 = (f32[1,2,2,64]{3,2,1,0:T(2,128)S(1)}, f32[1,2,2,64]{3,2,1,0:T(2,128)S(1)}, u32[]{:S(2)}, u32[]{:S(2)}) collective-permute-start(f32[1,2,2,64]{3,2,1,0:T(2,128)S(1)} %maximum_bitcast_fusion.10), channel_id=1, source_target_pairs={{0,8},{8,16},{16,24},{1,9},{9,17},{17,25},{2,10},{10,18},{18,26},{... | collective-permute-start | bytes 3080 | tf_op jit(solution)/shard_map/ppermute | solution.py:23
  308.9 28.4 %collective-permute-start.27 = (f32[2,64,384]{2,1,0:T(8,128)}, f32[2,64,384]{2,1,0:T(8,128)S(1)}, u32[]{:S(2)}, u32[]{:S(2)}) collective-permute-start(f32[2,64,384]{2,1,0:T(8,128)} %get-tuple-element.735), channel_id=1, source_target_pairs={{2,0},{4,2},{6,4},{3,1},{5,3},{7,5},{10,8},{12,10},{14,12},{11,9},... | collective-permute-start | bytes 589832 | tf_op jit(solution)/shard_map/ppermute | solution.py:13
  314.6 20.3 %collective-permute-start.20 = (f32[2,64,384]{2,1,0:T(8,128)}, f32[2,64,384]{2,1,0:T(8,128)}, u32[]{:S(2)}, u32[]{:S(2)}) collective-permute-start(f32[2,64,384]{2,1,0:T(8,128)} %get-tuple-element.734), channel_id=1, source_target_pairs={{0,8},{8,16},{16,24},{1,9},{9,17},{17,25},{2,10},{10,18},{18,26},{... | collective-permute-start | bytes 589832 | tf_op jit(solution)/shard_map/ppermute | solution.py:13
  316.6 18.3 %collective-permute-start.26 = (f32[2,64,384]{2,1,0:T(8,128)}, f32[2,64,384]{2,1,0:T(8,128)S(1)}, u32[]{:S(2)}, u32[]{:S(2)}) collective-permute-start(f32[2,64,384]{2,1,0:T(8,128)} %get-tuple-element.737), channel_id=1, source_target_pairs={{0,2},{2,4},{4,6},{1,3},{3,5},{5,7},{8,10},{10,12},{12,14},{9,11},... | collective-permute-start | bytes 589832 | tf_op jit(solution)/shard_map/ppermute | solution.py:13
  318.5 20.1 %collective-permute-start.25 = (f32[2,64,384]{2,1,0:T(8,128)}, f32[2,64,384]{2,1,0:T(8,128)S(1)}, u32[]{:S(2)}, u32[]{:S(2)}) collective-permute-start(f32[2,64,384]{2,1,0:T(8,128)} %get-tuple-element.736), channel_id=1, source_target_pairs={{8,0},{16,8},{24,16},{9,1},{17,9},{25,17},{10,2},{18,10},{26,18},{... | collective-permute-start | bytes 589832 | tf_op jit(solution)/shard_map/ppermute | solution.py:13
  392.1 17.4 %collective-permute-start.30 = (f32[1,2,2,64]{3,2,1,0:T(2,128)S(1)}, f32[1,2,2,64]{3,2,1,0:T(2,128)S(1)}, u32[]{:S(2)}, u32[]{:S(2)}) collective-permute-start(f32[1,2,2,64]{3,2,1,0:T(2,128)S(1)} %maximum_bitcast_fusion.13), channel_id=1, source_target_pairs={{8,0},{16,8},{24,16},{9,1},{17,9},{25,17},{10,2},{18,10},{26,18},{... | collective-permute-start | bytes 3080 | tf_op jit(solution)/shard_map/ppermute | solution.py:24
  395.5 18.9 %collective-permute-start.29 = (f32[1,2,2,64]{3,2,1,0:T(2,128)S(1)}, f32[1,2,2,64]{3,2,1,0:T(2,128)S(1)}, u32[]{:S(2)}, u32[]{:S(2)}) collective-permute-start(f32[1,2,2,64]{3,2,1,0:T(2,128)S(1)} %maximum_bitcast_fusion.12), channel_id=1, source_target_pairs={{0,8},{8,16},{16,24},{1,9},{9,17},{17,25},{2,10},{10,18},{18,26},{... | collective-permute-start | bytes 3080 | tf_op jit(solution)/shard_map/ppermute | solution.py:23
  400.0 28.3 %collective-permute-start.35 = (f32[2,64,384]{2,1,0:T(8,128)}, f32[2,64,384]{2,1,0:T(8,128)S(1)}, u32[]{:S(2)}, u32[]{:S(2)}) collective-permute-start(f32[2,64,384]{2,1,0:T(8,128)} %get-tuple-element.731), channel_id=1, source_target_pairs={{2,0},{4,2},{6,4},{3,1},{5,3},{7,5},{10,8},{12,10},{14,12},{11,9},... | collective-permute-start | bytes 589832 | tf_op jit(solution)/shard_map/ppermute | solution.py:13
  405.7 20.2 %collective-permute-start.28 = (f32[2,64,384]{2,1,0:T(8,128)}, f32[2,64,384]{2,1,0:T(8,128)}, u32[]{:S(2)}, u32[]{:S(2)}) collective-permute-start(f32[2,64,384]{2,1,0:T(8,128)} %get-tuple-element.730), channel_id=1, source_target_pairs={{0,8},{8,16},{16,24},{1,9},{9,17},{17,25},{2,10},{10,18},{18,26},{... | collective-permute-start | bytes 589832 | tf_op jit(solution)/shard_map/ppermute | solution.py:13
  407.6 18.3 %collective-permute-start.34 = (f32[2,64,384]{2,1,0:T(8,128)}, f32[2,64,384]{2,1,0:T(8,128)S(1)}, u32[]{:S(2)}, u32[]{:S(2)}) collective-permute-start(f32[2,64,384]{2,1,0:T(8,128)} %get-tuple-element.733), channel_id=1, source_target_pairs={{0,2},{2,4},{4,6},{1,3},{3,5},{5,7},{8,10},{10,12},{12,14},{9,11},... | collective-permute-start | bytes 589832 | tf_op jit(solution)/shard_map/ppermute | solution.py:13
  409.6 20.1 %collective-permute-start.33 = (f32[2,64,384]{2,1,0:T(8,128)}, f32[2,64,384]{2,1,0:T(8,128)S(1)}, u32[]{:S(2)}, u32[]{:S(2)}) collective-permute-start(f32[2,64,384]{2,1,0:T(8,128)} %get-tuple-element.732), channel_id=1, source_target_pairs={{8,0},{16,8},{24,16},{9,1},{17,9},{25,17},{10,2},{18,10},{26,18},{... | collective-permute-start | bytes 589832 | tf_op jit(solution)/shard_map/ppermute | solution.py:13
  483.2 16.7 %collective-permute-start.38 = (f32[1,2,2,64]{3,2,1,0:T(2,128)S(1)}, f32[1,2,2,64]{3,2,1,0:T(2,128)S(1)}, u32[]{:S(2)}, u32[]{:S(2)}) collective-permute-start(f32[1,2,2,64]{3,2,1,0:T(2,128)S(1)} %maximum_bitcast_fusion.15), channel_id=1, source_target_pairs={{8,0},{16,8},{24,16},{9,1},{17,9},{25,17},{10,2},{18,10},{26,18},{... | collective-permute-start | bytes 3080 | tf_op jit(solution)/shard_map/ppermute | solution.py:24
  485.9 18.9 %collective-permute-start.37 = (f32[1,2,2,64]{3,2,1,0:T(2,128)S(1)}, f32[1,2,2,64]{3,2,1,0:T(2,128)S(1)}, u32[]{:S(2)}, u32[]{:S(2)}) collective-permute-start(f32[1,2,2,64]{3,2,1,0:T(2,128)S(1)} %maximum_bitcast_fusion.14), channel_id=1, source_target_pairs={{0,8},{8,16},{16,24},{1,9},{9,17},{17,25},{2,10},{10,18},{18,26},{... | collective-permute-start | bytes 3080 | tf_op jit(solution)/shard_map/ppermute | solution.py:23
  491.1 26.3 %collective-permute-start.43 = (f32[2,64,384]{2,1,0:T(8,128)S(1)}, f32[2,64,384]{2,1,0:T(8,128)S(1)}, u32[]{:S(2)}, u32[]{:S(2)}) collective-permute-start(f32[2,64,384]{2,1,0:T(8,128)S(1)} %get-tuple-element.727), channel_id=1, source_target_pairs={{2,0},{4,2},{6,4},{3,1},{5,3},{7,5},{10,8},{12,10},{14,12},{11,9},... | collective-permute-start | bytes 589832 | tf_op jit(solution)/shard_map/ppermute | solution.py:13
  496.0 21.2 %collective-permute-start.36 = (f32[2,64,384]{2,1,0:T(8,128)}, f32[2,64,384]{2,1,0:T(8,128)S(1)}, u32[]{:S(2)}, u32[]{:S(2)}) collective-permute-start(f32[2,64,384]{2,1,0:T(8,128)} %get-tuple-element.726), channel_id=1, source_target_pairs={{0,8},{8,16},{16,24},{1,9},{9,17},{17,25},{2,10},{10,18},{18,26},{... | collective-permute-start | bytes 589832 | tf_op jit(solution)/shard_map/ppermute | solution.py:13
  498.0 19.2 %collective-permute-start.42 = (f32[2,64,384]{2,1,0:T(8,128)}, f32[2,64,384]{2,1,0:T(8,128)S(1)}, u32[]{:S(2)}, u32[]{:S(2)}) collective-permute-start(f32[2,64,384]{2,1,0:T(8,128)} %get-tuple-element.729), channel_id=1, source_target_pairs={{0,2},{2,4},{4,6},{1,3},{3,5},{5,7},{8,10},{10,12},{12,14},{9,11},... | collective-permute-start | bytes 589832 | tf_op jit(solution)/shard_map/ppermute | solution.py:13
  499.9 18.0 %collective-permute-start.41 = (f32[2,64,384]{2,1,0:T(8,128)S(1)}, f32[2,64,384]{2,1,0:T(8,128)S(1)}, u32[]{:S(2)}, u32[]{:S(2)}) collective-permute-start(f32[2,64,384]{2,1,0:T(8,128)S(1)} %get-tuple-element.728), channel_id=1, source_target_pairs={{8,0},{16,8},{24,16},{9,1},{17,9},{25,17},{10,2},{18,10},{26,18},{... | collective-permute-start | bytes 589832 | tf_op jit(solution)/shard_map/ppermute | solution.py:13
  536.2 16.8 %collective-permute-start.48 = (f32[4,1,2,64]{3,2,1,0:T(2,128)S(1)}, f32[4,1,2,64]{3,2,1,0:T(2,128)S(1)}, u32[]{:S(2)}, u32[]{:S(2)}) collective-permute-start(f32[4,1,2,64]{3,2,1,0:T(2,128)S(1)} %get-tuple-element.815), channel_id=1, source_target_pairs={{2,0},{4,2},{6,4},{3,1},{5,3},{7,5},{10,8},{12,10},{14,12},{11,9},... | collective-permute-start | bytes 6152 | tf_op jit(solution)/shard_map/ppermute | solution.py:24
  540.2 18.9 %collective-permute-start.51 = (f32[2,64,384]{2,1,0:T(8,128)S(1)}, f32[2,64,384]{2,1,0:T(8,128)S(1)}, u32[]{:S(2)}, u32[]{:S(2)}) collective-permute-start(f32[2,64,384]{2,1,0:T(8,128)S(1)} %get-tuple-element.724), channel_id=1, source_target_pairs={{2,0},{4,2},{6,4},{3,1},{5,3},{7,5},{10,8},{12,10},{14,12},{11,9},... | collective-permute-start | bytes 589832 | tf_op jit(solution)/shard_map/ppermute | solution.py:13
  542.1 16.8 %collective-permute-start.44 = (f32[2,64,384]{2,1,0:T(8,128)S(1)}, f32[2,64,384]{2,1,0:T(8,128)S(1)}, u32[]{:S(2)}, u32[]{:S(2)}) collective-permute-start(f32[2,64,384]{2,1,0:T(8,128)S(1)} %get-tuple-element.722), channel_id=1, source_target_pairs={{0,8},{8,16},{16,24},{1,9},{9,17},{17,25},{2,10},{10,18},{18,26},{... | collective-permute-start | bytes 589832 | tf_op jit(solution)/shard_map/ppermute | solution.py:13
  (26 other events, 246.0 us)
